TPU v7x, 256 devices: a 2x2x32 block of a 4x8x32 slice. The times are simulated.
256 devices in a mesh: groups: 4 (over y, x), dom: 64 (over z, core).
Axes of the slice: x: 2, y: 2, z: 32, core: 2. Of those that a mesh axis runs over, the one named last changes fastest.
The devices are a block of a 4x8x32 slice.
Arguments:
- particles: bfloat16 [8192, 4096], P(('groups', 'dom')), parts along dimension 0, may hold values from -5 to 5
- dataset: bfloat16 [16384, 4096], P(('groups', 'dom')), parts along dimension 0, may hold values from -0.09375 to 0.09375
- labels: int32 [16384], P(('groups', 'dom')), parts along dimension 0, may hold values 0 or 1
- batch_index: int32 [4096], P(('groups', 'dom')), parts along dimension 0, may hold values from 0 to 4095, as said below
Outputs:
- driving: float32 [8192, 4096], P(('groups', 'dom')), parts along dimension 0
- spreading: float32 [8192, 4096], P(('groups', 'dom')), parts along dimension 0
There are 4 independent parts, one for each index of `groups`. A program takes and returns all parts, laid end to end along the dimension named above; each array names one. Nothing has to cross between parts.
Inputs may be any that keep to these rules, and one draw needn't show every extreme that they name: `batch_index`: entry b names a row of block b // 16 of the dataset, that is a row from (b // 16) * 64 to (b // 16 + 1) * 64 - 1; rows may repeat.
All inputs are finite; a program needn't handle non-finite values. No bound on the sum of `labels` on one device may be relied on, other than what follows from the above.
Results may differ from a plain program's by a relative error of at most 0.0003.
Values may be sent and summed in bfloat16 or wider, within the bound.
A program may use at most 128 MiB of HBM per device.

v0:
```python
import jax
import jax.numpy as jnp
from jax import lax
from jax.sharding import PartitionSpec as P

D = 4096


prior_precision = 1.0


def in_one_piece(arrays, axis, dim, along):
    columns = [a.reshape(*a.shape[:along], -1) for a in arrays]
    both = jnp.concatenate(columns, axis=along)
    filled, at, done = (lax.all_gather(both, axis, axis=dim, tiled=True), 0, [])
    for a, column in zip(arrays, columns):
        section = filled[..., at : at + column.shape[along]]
        done.append(section.reshape(*section.shape[:along], *a.shape[along:]))
        at += column.shape[along]
    return tuple(done)


def sent_together(arrays, axis, dim, along):
    ends, at = ([], 0)
    for a in arrays[:-1]:
        at += a.shape[along]
        ends.append(at)
    both = jnp.concatenate(arrays, axis=along)
    return tuple(jnp.split(lax.all_gather(both, axis, axis=dim, tiled=True), ends, axis=along))


def per_device(particles, dataset, labels, batch_index):
    own_rows = dataset.shape[0]
    local_index = batch_index - lax.axis_index("dom") * own_rows
    rows = jnp.take(dataset, local_index, axis=0)
    targets = jnp.take(labels, local_index).astype(jnp.bfloat16)
    particles_f = particles.astype(jnp.float32)
    ratio = float(own_rows) / float(batch_index.shape[0])
    all_rows, all_targets = in_one_piece((rows, targets), "dom", 0, 1)
    logits = lax.dot_general(
        particles, all_rows, (((1,), (1,)), ((), ())), preferred_element_type=jnp.float32
    )
    misfit = (all_targets.astype(jnp.float32)[None, :] - jax.nn.sigmoid(logits)).astype(
        jnp.bfloat16
    )
    pulled = jnp.dot(misfit, all_rows, preferred_element_type=jnp.float32)
    scores = (-prior_precision * particles_f + ratio * pulled).astype(jnp.bfloat16)
    squares = jnp.sum(particles_f * particles_f, axis=1)
    kernel_scale = 0.25 * D
    others, other_scores = sent_together((particles, scores), "dom", 0, 1)
    others_f = others.astype(jnp.float32)
    other_squares = jnp.sum(others_f * others_f, axis=1)
    cross = lax.dot_general(
        particles, others, (((1,), (1,)), ((), ())), preferred_element_type=jnp.float32
    )
    dist = squares[:, None] + other_squares[None, :] - 2.0 * cross
    kernel = jnp.exp(-dist / kernel_scale)
    kernel_b = kernel.astype(jnp.bfloat16)
    drive = jnp.dot(kernel_b, other_scores, preferred_element_type=jnp.float32)
    pull = jnp.dot(kernel_b, others, preferred_element_type=jnp.float32)
    rowsum = jnp.sum(kernel, axis=1)
    drive, pull, rowsum = (drive, pull, rowsum)
    total = float(particles.shape[0] * lax.axis_size("dom"))
    driving = drive / total
    spreading = (particles_f * rowsum[:, None] - pull) / total
    return (driving, spreading)


def solution(mesh):
    placed = (
        P(("groups", "dom"), None),
        P(("groups", "dom"), None),
        P(("groups", "dom")),
        P(("groups", "dom")),
    )
    return jax.shard_map(
        per_device,
        mesh=mesh,
        in_specs=placed,
        out_specs=(P(("groups", "dom"), None), P(("groups", "dom"), None)),
        check_vma=False,
    )
```

profile of v0, /device:TPU:37, one launch (start us, length us, event | category | flops | bytes accessed | tf_op | source)
XLA Modules:
  0.0 410.5 jit_solution(13735790966799115598)
XLA Ops:
  7.2 0.0 copy-start
  7.2 0.0 copy-start.1
  7.2 0.1 all-gather.3.cloned.1.call-start
  7.3 0.7 compare_and_fusion
  8.0 1.3 gather_fusion.1
  9.3 0.1 copy.7
  9.4 0.0 copy-done
  9.4 0.6 gather_fusion
  10.1 0.1 broadcast_select_fusion
  10.2 0.7 pad_maximum_fusion.1
  10.8 0.1 all-gather.3.cloned.1.call-update
  10.9 0.1 all-gather.5.cloned.1.call-start
  11.0 152.0 %all-gather.3.cloned.1.call-done = bf16[1024,4097]{1,0:T(8,128)(2,1)} async-done(((bf16[16,4097]{1,0:T(8,128)(2,1)}), bf16[1024,4097]{1,0:T(8,128)(2,1)}) %all-gather.3.cloned.1.call-update) | async-done | bytes 8390672 | tf_op jit(solution)/shard_map/all_gather | solution.py:15
  162.9 1.1 convert_reduce_fusion
  164.0 11.3 %fusion.25 = bf16[32,4096]{1,0:T(8,128)(2,1)S(1)} fusion(bf16[1024,4097]{1,0:T(8,128)(2,1)} %all-gather.3.cloned.1.call-done, bf16[32,4096]{1,0:T(8,128)(2,1)} %param.4, f32[1024]{0:T(1024)S(1)} %convert_reduce_fusion), kind=kOutput, calls=%fused_computation.18 | convolution fusion | flops 537690112 | bytes 17567744 | tf_op jit(solution)/shard_map/dot_general | solution.py:46
  175.4 0.0 copy-done.1
  175.4 0.8 pad_maximum_fusion
  176.2 0.1 all-gather.5.cloned.1.call-update
  176.3 0.2 fusion.66
  176.4 194.8 %all-gather.5.cloned.1.call-done = bf16[2048,8192]{1,0:T(8,128)(2,1)} async-done(((bf16[32,8192]{1,0:T(8,128)(2,1)}), bf16[2048,8192]{1,0:T(8,128)(2,1)}) %all-gather.5.cloned.1.call-update) | async-done | bytes 33554448 | tf_op jit(solution)/shard_map/all_gather | solution.py:29
  371.3 7.2 %multiply_reduce_fusion = f32[2048]{0:T(1024)S(1)} fusion(bf16[2048,8192]{1,0:T(8,128)(2,1)} %all-gather.5.cloned.1.call-done), kind=kLoop, calls=%fused_computation.2 | loop fusion | flops 25163776 | bytes 16785408 | tf_op jit(solution)/shard_map/reduce_sum | solution.py:52
  378.5 8.8 %fusion.72 = (f32[32]{0:T(128)S(1)}, bf16[32,2048]{1,0:T(8,128)(2,1)S(1)}) fusion(bf16[32,4096]{1,0:T(8,128)(2,1)S(1)} %copy-done.1, bf16[2048,8192]{1,0:T(8,128)(2,1)} %all-gather.5.cloned.1.call-done, f32[2048]{0:T(1024)S(1)} %multiply_reduce_fusion, f32[32]{0:T(128)S(1)} %fusion.66), kind=kOutput, calls=%fused_computation.48 | convolution fusion | flops 537329664 | bytes 17178880 | tf_op jit(solution)/shard_map/dot_general | solution.py:53
  387.3 8.1 %fusion.19 = f32[32,4096]{1,0:T(8,128)} fusion(bf16[2048,8192]{1,0:T(8,128)(2,1)} %all-gather.5.cloned.1.call-done, bf16[32,2048]{1,0:T(8,128)(2,1)S(1)} %get-tuple-element.5), kind=kOutput, calls=%fused_computation.16 | convolution fusion | flops 537001984 | bytes 17432576 | tf_op jit(solution)/shard_map/dot_general | solution.py:59
  395.4 8.2 %fusion.16 = f32[32,4096]{1,0:T(8,128)} fusion(bf16[2048,8192]{1,0:T(8,128)(2,1)} %all-gather.5.cloned.1.call-done, bf16[32,4096]{1,0:T(8,128)(2,1)S(1)} %copy-done.1, f32[32]{0:T(128)S(1)} %get-tuple-element.4, bf16[32,2048]{1,0:T(8,128)(2,1)S(1)} %get-tuple-element.5), kind=kOutput, calls=%fused_computation.15 | convolution fusion | flops 537395200 | bytes 17694848 | tf_op jit(solution)/shard_map/dot_general | solution.py:60
  (2 shorter events, 0.0 us)
Async XLA Ops:
  7.2 2.3 copy-start
  7.2 168.2 %copy-start.1 = (bf16[32,4096]{1,0:T(8,128)(2,1)S(1)}, bf16[32,4096]{1,0:T(8,128)(2,1)}, u32[]{:S(2)}) copy-start(bf16[32,4096]{1,0:T(8,128)(2,1)} %param.4) | copy-start | bytes 786436
  7.2 155.7 %all-gather.3.cloned.1.call-start = ((), (), s32[]{:S(2)}) async-start(), calls=%async_computation | async-start | bytes 8785920 | tf_op jit(solution)/shard_map/all_gather | solution.py:15
  10.9 360.4 %all-gather.5.cloned.1.call-start = ((), (), s32[]{:S(2)}) async-start(), calls=%async_computation.1 | async-start | bytes 34078720 | tf_op jit(solution)/shard_map/all_gather | solution.py:29
Sparse Core Ops, SparseCore 0:
  11.0 151.8 all-gather.2
  176.4 194.8 all-gather.4
where the time goes:
time: 411 us
  waiting for transfers between devices  347 us (84%)
  matrix products  36.6 us (9%)
  between operations  14.1 us (3%)
  other arithmetic  10.8 us (3%)
    all_gather x1, waiting for transfers between devices, sent_together(): lax.all_gather(both, axis, axis=dim, tiled=True)  195 us
    all_gather x1, waiting for transfers between devices, in_one_piece(): filled, at, done = (lax.all_gather(both, axis, axis=dim, tiled=True), 0, [])  152 us
    dot_general x1, matrix products, per_device(): pulled = jnp.dot(misfit, all_rows, preferred_element_type=jnp.float32)  11.3 us
    dot_general x1, matrix products, per_device(): lax.dot_general(particles, others, (((1,), (1,)), ((), ())), preferred_el...  8.84 us
    dot_general x1, matrix products, per_device(): pull = jnp.dot(kernel_b, others, preferred_element_type=jnp.float32)  8.25 us
  transfers between devices with their start and end apart: 2, of which 2 were waited for; matrix products, arithmetic and copies ran while one was open for 0% of the time, Pallas kernels for 0%

commit v1 on v0

v1 whole, which is shorter than its diff:
```python
import functools

import jax
import jax.numpy as jnp
from jax import lax
from jax.experimental import pallas as pl
from jax.experimental.pallas import tpu as pltpu
from jax.sharding import PartitionSpec as P

KERNEL_SCALE_PER_FEATURE = 0.25
PRIOR_PRECISION = 1.0
LANES = 128
CHUNKS = 4
PER_GROUP = 4
MIXED = 4
MESH = pl.DeviceIdType.MESH
BF16, F32 = jnp.bfloat16, jnp.float32
NT = (((1,), (1,)), ((), ()))


def ring_kernel(
    chips,
    p_hbm,
    d_hbm,
    labels,
    index,
    driving,
    spreading,
    rows,
    parts,
    mine,
    data,
    misfit,
    kern,
    sums,
    inbox,
    rowsum,
    rowsum_in,
    target_row,
    squares,
    local_sems,
    row_recv,
    row_send,
    row_sib_recv,
    row_sib_send,
    part_recv,
    part_send,
    mine_recv,
    mine_send,
    sums_recv,
    sums_send,
    rowsum_recv,
    rowsum_send,
):
    dom = lax.axis_index("dom")
    core = lax.rem(dom, 2)
    z = lax.div(dom, 2)
    right = lax.rem(z + 1, chips) * 2 + core
    left = lax.rem(z + chips - 1, chips) * 2 + core
    sibling = dom + 1 - 2 * core

    d = p_hbm.shape[1]
    np_own = p_hbm.shape[0]
    nb_own = index.shape[0]
    own_rows = d_hbm.shape[0]
    half = chips * nb_own
    nb = 2 * half
    wide = rows.shape[1]
    last = chips // 2
    groups = chips // PER_GROUP
    j_size = PER_GROUP * np_own
    total = float(2 * chips * np_own)
    ratio = float(own_rows) / float(nb_own)
    scale = KERNEL_SCALE_PER_FEATURE * d

    def slot_of(step, direction):
        return jnp.clip(2 * step - 1 + direction, 0, chips - 1)

    def row_chunk(slot, q):
        width = d // CHUNKS
        start = q * width
        if q == CHUNKS - 1:
            width += wide - d
        at = pl.multiple_of(slot * nb_own, nb_own)
        return rows.at[pl.ds(at, nb_own), pl.ds(start, width)]

    def part_chunk(slot, q):
        high, width = np_own // 2, d // 2
        at = pl.multiple_of(slot * np_own + (q // 2) * high, high)
        col = pl.multiple_of((q % 2) * width, width)
        return parts.at[pl.ds(at, high), pl.ds(col, width)]

    def hop(chunk, recv, send, step, direction, q):
        fixed = isinstance(step, int)
        src = 0 if fixed and step == 1 else slot_of(step - 1, direction)
        end = fixed and step == last
        return pltpu.make_async_remote_copy(
            src_ref=chunk(src, q),
            dst_ref=chunk(slot_of(step, direction), q),
            send_sem=send.at[2 * end + direction],
            recv_sem=recv.at[(direction * last + step - 1) * CHUNKS + q],
            device_id={"dom": right if direction == 0 else left},
            device_id_type=MESH,
        )

    row_hop = functools.partial(hop, row_chunk, row_recv, row_send)
    part_hop = functools.partial(hop, part_chunk, part_recv, part_send)

    def kept(direction, q):
        return q < CHUNKS // 2 if direction == 0 else q >= CHUNKS // 2

    def row_to_sibling(slot):
        at = pl.multiple_of(slot * nb_own, nb_own)
        return pltpu.make_async_remote_copy(
            src_ref=rows.at[pl.ds(at, nb_own), :],
            dst_ref=rows.at[pl.ds(half + at, nb_own), :],
            send_sem=row_sib_send,
            recv_sem=row_sib_recv,
            device_id={"dom": sibling},
            device_id_type=MESH,
        )

    load_data = pltpu.make_async_copy(d_hbm, data, local_sems.at[0])
    load_part = pltpu.make_async_copy(p_hbm, parts.at[pl.ds(0, np_own), :], local_sems.at[1])
    load_mine = pltpu.make_async_copy(p_hbm, mine.at[pl.ds(0, np_own), :], local_sems.at[2])
    load_part.start()
    load_data.start()
    load_mine.start()
    barrier = pltpu.get_barrier_semaphore()
    for peer in (left, right, sibling):
        pl.semaphore_signal(barrier, inc=1, device_id={"dom": peer}, device_id_type=MESH)

    load_part.wait()
    pl.semaphore_wait(barrier, 3)
    def part_mix(at):
        step, q = lax.div(at, CHUNKS), lax.rem(at, CHUNKS)

        @pl.when(step > 0)
        def _():
            for direction in (0, 1):
                part_hop(step, direction, q).wait_recv()

        for direction in (0, 1):
            part_hop(step + 1, direction, q).start()

    part_mix(jnp.int32(0))

    lane = lax.broadcasted_iota(jnp.int32, (nb_own, LANES), 1)
    sub = lax.broadcasted_iota(jnp.int32, (nb_own, LANES), 0)
    pick = jnp.zeros((nb_own, LANES), F32)
    target = jnp.zeros((nb_own, LANES), F32)
    for r in range(nb_own):
        at = lax.rem(index[r], own_rows)
        label = labels[at].astype(F32)
        pick = jnp.where((sub == r) & (lane == at), 1.0, pick)
        target = jnp.where((sub == r) & (lane == 0), label, target)
    load_data.wait()
    rows[pl.ds(0, nb_own), pl.ds(d, LANES)] = target.astype(BF16)
    rows[pl.ds(0, nb_own), pl.ds(0, d)] = jnp.dot(
        pick[:, :own_rows].astype(BF16), data[...], preferred_element_type=F32
    ).astype(BF16)

    for q in range(CHUNKS):
        row_hop(1, 0, q).start()
        row_hop(1, 1, q).start()
    swap = pltpu.make_async_remote_copy(
        src_ref=mine.at[pl.ds(0, np_own), :],
        dst_ref=mine.at[pl.ds(np_own, np_own), :],
        send_sem=mine_send,
        recv_sem=mine_recv,
        device_id={"dom": sibling},
        device_id_type=MESH,
    )
    row_to_sibling(0).start()
    load_mine.wait()
    swap.start()
    sums[...] = jnp.zeros_like(sums)
    rowsum[...] = jnp.zeros_like(rowsum)

    stride = CHUNKS // MIXED

    def mix_at(step):
        @pl.when(lax.rem(step, stride) == 0)
        def _():
            part_mix(lax.div(step, stride))

    def row_step(step, carry):
        for q in range(CHUNKS):
            for direction in (0, 1):
                row_hop(step, direction, q).wait_recv()
                row_hop(step + 1, direction, q).start()
        mix_at(step)
        row_to_sibling(2 * step - 1).start()
        row_to_sibling(2 * step).start()
        return carry

    lax.fori_loop(1, last - 1, row_step, 0)
    for q in range(CHUNKS):
        for direction in (0, 1):
            row_hop(last - 1, direction, q).wait_recv()
            if kept(direction, q):
                row_hop(last, direction, q).start()
    mix_at(jnp.int32(last - 1))
    row_to_sibling(2 * last - 3).start()
    row_to_sibling(2 * last - 2).start()
    for q in range(CHUNKS):
        row_hop(last, 0 if kept(0, q) else 1, q).wait_recv()
    row_to_sibling(chips - 1).start()
    lax.fori_loop((last - 1) // stride + 1, CHUNKS * (MIXED + 1), lambda at, c: (part_mix(at), c)[1], 0)
    swap.wait_recv()
    m = mine[...].astype(F32)
    squares[...] = jnp.broadcast_to(jnp.sum(m * m, axis=1, keepdims=True), squares.shape)
    pltpu.make_async_remote_copy(
        src_ref=rows.at[pl.ds(0, half), :],
        dst_ref=rows.at[pl.ds(half, half), :],
        send_sem=row_sib_send,
        recv_sem=row_sib_recv,
        device_id={"dom": sibling},
        device_id_type=MESH,
    ).wait()
    first = (lax.broadcasted_iota(jnp.int32, (8, LANES), 1) == 0).astype(BF16)
    target_row[...] = lax.dot_general(
        first, rows[:, pl.ds(d, LANES)], NT, preferred_element_type=F32
    )

    nbq, dq = nb // CHUNKS, d // CHUNKS

    def group_rows(group, many=1):
        return pl.ds(pl.multiple_of(group * j_size, j_size), many * j_size)

    def kernel_block(group, many=1):
        for i in range(many):
            block = parts[group_rows(group + i), :]
            cross = lax.dot_general(mine[...], block, NT, preferred_element_type=F32)
            folded = jnp.zeros((j_size, LANES), F32)
            for k in range(d // LANES):
                piece = parts[group_rows(group + i), pl.ds(k * LANES, LANES)].astype(F32)
                folded = folded + piece * piece
            others = jnp.sum(folded.T, axis=0, keepdims=True)
            dist = squares[:, :1] + others - 2.0 * cross
            kernel = jnp.exp(-dist / scale)
            kern[:, pl.ds(i * j_size, j_size)] = kernel.astype(BF16)
            rowsum[...] += kernel

    def misfit_block(group, q, many=1):
        logits = lax.dot_general(
            parts[group_rows(group, many), :],
            rows[pl.ds(q * nbq, nbq), pl.ds(0, d)],
            NT,
            preferred_element_type=F32,
        )
        misfit[pl.ds(0, many * j_size), pl.ds(q * nbq, nbq)] = (
            target_row[:1, pl.ds(q * nbq, nbq)] - jax.nn.sigmoid(logits)
        ).astype(BF16)

    def sums_block(group, q, many=1):
        cols = pl.ds(q * dq, dq)
        own = pl.ds(0, many * j_size)
        pulled = jnp.dot(misfit[own, :], rows[:, cols], preferred_element_type=F32)
        block = parts[group_rows(group, many), cols]
        scores = (-PRIOR_PRECISION * block.astype(F32) + ratio * pulled).astype(BF16)
        weights = kern[:, own]
        sums[0, :, cols] += jnp.dot(weights, scores, preferred_element_type=F32)
        sums[1, :, cols] += jnp.dot(weights, block, preferred_element_type=F32)

    ahead = MIXED // 2

    def part_step(group, carry):
        more = group < groups - 1
        double = group <= 2 * ahead - 2

        def work(block):
            pl.when(double)(lambda: block(2 * (group - ahead), 2))
            pl.when(jnp.logical_not(double))(lambda: block(group - 1, 1))

        for q in range(CHUNKS):
            step = 2 * group + 1
            for direction in (0, 1):
                part_hop(step, direction, q).wait_recv()
                if kept(direction, q):
                    part_hop(step + 1, direction, q).start()
                else:
                    pl.when(more)(part_hop(step + 1, direction, q).start)

            if q == 0:
                work(kernel_block)
            work(lambda at, many: misfit_block(at, q, many))

        for q in range(CHUNKS):
            step = 2 * group + 2
            for direction in (0, 1):

                def pass_on():
                    part_hop(step + 1, direction, q).start()

                if kept(direction, q):
                    part_hop(step, direction, q).wait_recv()
                    pl.when(more)(pass_on)
                else:

                    @pl.when(more)
                    def _():
                        part_hop(step, direction, q).wait_recv()
                        pass_on()

            work(lambda at, many: sums_block(at, q, many))

        return carry

    lax.fori_loop(ahead, groups, part_step, 0)

    def sums_hop(kind, q):
        cols = pl.ds(q * dq, dq)
        return pltpu.make_async_remote_copy(
            src_ref=sums.at[kind, pl.ds(np_own, np_own), cols],
            dst_ref=inbox.at[kind, :, cols],
            send_sem=sums_send.at[kind * CHUNKS + q],
            recv_sem=sums_recv.at[kind * CHUNKS + q],
            device_id={"dom": sibling},
            device_id_type=MESH,
        )

    rowsum_hop = pltpu.make_async_remote_copy(
        src_ref=rowsum.at[pl.ds(np_own, np_own), :],
        dst_ref=rowsum_in,
        send_sem=rowsum_send,
        recv_sem=rowsum_recv,
        device_id={"dom": sibling},
        device_id_type=MESH,
    )
    kernel_block(groups - 1)
    for q in range(CHUNKS):
        misfit_block(groups - 1, q)
        if q == 0:
            rowsum_hop.start()
    for q in range(CHUNKS):
        sums_block(groups - 1, q)
        if q > 0:
            sums_hop(0, q - 1).start()
            sums_hop(1, q - 1).start()
    rowsum_hop.wait_recv()
    own_rowsum = jnp.sum(
        rowsum[pl.ds(0, np_own), :] + rowsum_in[...], axis=1, keepdims=True
    )
    squares[pl.ds(0, np_own), :] = jnp.broadcast_to(own_rowsum, (np_own, LANES))
    sums_hop(0, CHUNKS - 1).start()
    sums_hop(1, CHUNKS - 1).start()
    for q in range(CHUNKS):
        cols = pl.ds(q * dq, dq)
        sums_hop(0, q).wait_recv()
        sums_hop(1, q).wait_recv()
        own = pl.ds(0, np_own)
        driving[:, cols] = (sums[0, own, cols] + inbox[0, :, cols]) / total
        pull = sums[1, own, cols] + inbox[1, :, cols]
        spreading[:, cols] = (mine[own, cols].astype(F32) * squares[own, :1] - pull) / total

    for q in range(CHUNKS):
        sums_hop(0, q).wait_send()
        sums_hop(1, q).wait_send()
    rowsum_hop.wait_send()
    swap.wait_send()
    for direction, peer in ((0, right), (1, left)):
        sent = (last - 1) * nb_own
        middle = d // 2
        cols = pl.ds(0, middle) if direction == 0 else pl.ds(middle, wide - middle)
        for end, region in enumerate(
            (rows.at[pl.ds(0, sent), :], rows.at[pl.ds(0, nb_own), cols])
        ):
            pltpu.make_async_remote_copy(
                src_ref=region,
                dst_ref=region,
                send_sem=row_send.at[2 * end + direction],
                recv_sem=row_recv.at[0],
                device_id={"dom": peer},
                device_id_type=MESH,
            ).wait_send()
        sent = (2 * last - 1) * np_own // 2
        pltpu.make_async_remote_copy(
            src_ref=parts.at[pl.ds(0, sent), :],
            dst_ref=parts.at[pl.ds(0, sent), :],
            send_sem=part_send.at[direction],
            recv_sem=part_recv.at[0],
            device_id={"dom": peer},
            device_id_type=MESH,
        ).wait_send()


def per_device(chips, particles, dataset, labels, batch_index):
    np_own, d = particles.shape
    nb_own = batch_index.shape[0]
    nb = 2 * chips * nb_own
    j_size = PER_GROUP * np_own
    hops = 2 * (chips // 2) * CHUNKS
    dma = pltpu.SemaphoreType.DMA
    out = jax.ShapeDtypeStruct((np_own, d), F32)
    return pl.pallas_call(
        functools.partial(ring_kernel, chips),
        out_shape=(out, out),
        in_specs=[
            pl.BlockSpec(memory_space=pl.ANY),
            pl.BlockSpec(memory_space=pl.ANY),
            pl.BlockSpec(memory_space=pltpu.SMEM),
            pl.BlockSpec(memory_space=pltpu.SMEM),
        ],
        out_specs=[pl.BlockSpec(memory_space=pltpu.VMEM)] * 2,
        scratch_shapes=[
            pltpu.VMEM((nb, d + LANES), BF16),
            pltpu.VMEM((chips * np_own, d), BF16),
            pltpu.VMEM((2 * np_own, d), BF16),
            pltpu.VMEM(dataset.shape, BF16),
            pltpu.VMEM((2 * j_size, nb), BF16),
            pltpu.VMEM((2 * np_own, 2 * j_size), BF16),
            pltpu.VMEM((2, 2 * np_own, d), F32),
            pltpu.VMEM((2, np_own, d), F32),
            pltpu.VMEM((2 * np_own, j_size), F32),
            pltpu.VMEM((np_own, j_size), F32),
            pltpu.VMEM((8, nb), F32),
            pltpu.VMEM((2 * np_own, LANES), F32),
            dma((3,)),
            dma((hops,)),
            dma((4,)),
            dma,
            dma,
            dma((hops,)),
            dma((2,)),
            dma,
            dma,
            dma((2 * CHUNKS,)),
            dma((2 * CHUNKS,)),
            dma,
            dma,
        ],
        compiler_params=pltpu.CompilerParams(collective_id=0, has_side_effects=True),
    )(particles, dataset, labels, batch_index)


def solution(mesh):
    placed = (
        P(("groups", "dom"), None),
        P(("groups", "dom"), None),
        P(("groups", "dom")),
        P(("groups", "dom")),
    )
    return jax.shard_map(
        functools.partial(per_device, mesh.shape["dom"] // 2),
        mesh=mesh,
        in_specs=placed,
        out_specs=(P(("groups", "dom"), None), P(("groups", "dom"), None)),
        check_vma=False,
    )
```

time: 411 us -> 178 us (0.43)
  waiting for transfers between devices: 347 us -> 0 us
  Pallas kernels: 0 us -> 174 us
  matrix products: 36.6 us -> 0 us
  between operations: 14.1 us -> 0.65 us
  other arithmetic: 10.8 us -> 0 us
    all_gather x2 -> x0, waiting for transfers between devices: 347 us -> none  [the longest x1 195 us: sent_together(): lax.all_gather(both, axis, axis=dim, tiled=True)]
    pallas_call x0 -> x1, Pallas kernels: none -> 174 us  [per_device(): pl.pallas_call(functools.partial(ring_kernel, chips), out_shape=(out, out...]
    dot_general x4 -> x0, matrix products: 36.6 us -> none  [the longest x1 11.3 us: per_device(): pulled = jnp.dot(misfit, all_rows, preferred_element_type=jnp.float32)]
    reduce_sum x2 -> x0, other arithmetic: 7.37 us -> none  [the longest x1 7.2 us: per_device(): other_squares = jnp.sum(others_f * others_f, axis=1)]
  transfers between devices with their start and end apart: 2 -> 0, of which waited for: 2 -> 0; matrix products, arithmetic and copies ran while one was open for 0% -> 0% of each run, Pallas kernels for 0% -> 0%
where the time goes in v1:
time: 178 us
  Pallas kernels  174 us (98%)
  local copies, waits for them, and re-layouts  2.72 us (2%)
    pallas_call x1, Pallas kernels, per_device(): pl.pallas_call(functools.partial(ring_kernel, chips), out_shape=(out, out...  174 us

profile of v1, /device:TPU:37, one launch (start us, length us, event | category | flops | bytes accessed | tf_op | source)
XLA Modules:
  0.0 177.6 jit_solution(12474339030190978140)
XLA Ops:
  0.6 174.3 %shard_map.59 = (f32[32,4096]{1,0:T(8,128)}, f32[32,4096]{1,0:T(8,128)}) custom-call(bf16[32,4096]{1,0:T(8,128)(2,1)} %p_hbm.1, bf16[64,4096]{1,0:T(8,128)(2,1)} %d_hbm.1, s32[64]{0:T(128)} %labels.1, s32[16]{0:T(128)} %index.1), custom_call_target="tpu_custom_call" | custom-call | tf_op jit(solution)/shard_map/pallas_call | solution.py:396
  174.9 0.0 copy-start
  174.9 1.9 %copy.8 = f32[32,4096]{1,0:T(8,128)} copy(f32[32,4096]{1,0:T(8,128)} %get-tuple-element.4) | data formatting | bytes 1048576
  176.8 0.0 copy-done
  176.8 0.8 copy.9
Async XLA Ops:
  174.9 1.9 %copy-start = (f32[32,4096]{1,0:T(8,128)S(1)}, f32[32,4096]{1,0:T(8,128)}, u32[]{:S(2)}) copy-start(f32[32,4096]{1,0:T(8,128)} %get-tuple-element.5) | copy-start | bytes 1572868
